TPU v7x, 32 devices: a whole 2x2x4 slice. The times are simulated.
32 devices in a mesh: row: 4 (over y, core), col: 8 (over z, x).
Axes of the slice: x: 2, y: 2, z: 4, core: 2. Of those that a mesh axis runs over, the one named last changes fastest.
Arguments:
- density: float32 [4096, 32768], P('row', 'col'), may hold values from 0 to 1
- design_mask: int32 [32, 256], P('row', 'col'), may hold values 0 or 1
- rebalance: int32 [8192], replicated, may hold values from 0 to 8191, as said below
Outputs:
- balanced: bfloat16 [8192, 128, 128], P(('row', 'col'))
- constraint: float32 [], replicated
Inputs may be any that keep to these rules, and one draw needn't show every extreme that they name: `rebalance`: A permutation of the 8192 block numbers. Of the blocks that one device holds, the ones that land among one device's output blocks number exactly 8 or none.
All inputs are finite; a program needn't handle non-finite values. No bound on the sum of `design_mask` on one device may be relied on, other than what follows from the above.
Results may differ from a plain program's by a relative error of at most 0.001.
Values may be sent and summed in bfloat16 or wider, within the bound.
A program may use at most 192 MiB of HBM per device.

v0:
```python
import jax
import jax.numpy as jnp
from jax import lax
from jax.sharding import PartitionSpec as P

BS = 128
RADIUS = 16


SHARPNESS = 32.0
THRESHOLD = 0.5
VOLUME_TARGET = 0.4


def with_halo(shard, sides, width):
    for axis, dim in sides:
        devices, length = (lax.axis_size(axis), shard.shape[dim])
        up = [(i, (i + 1) % devices) for i in range(devices - 1)]
        down = [(j, i) for i, j in up]
        last = lax.slice_in_dim(shard, length - width, length, axis=dim)
        initial = lax.slice_in_dim(shard, 0, width, axis=dim)
        before = lax.ppermute(last, axis, up)
        after = lax.ppermute(initial, axis, down)
        shard = jnp.concatenate([before, shard, after], axis=dim)
    return shard


def filter_taps():
    sigma = RADIUS / 4.0
    offsets = jnp.arange(2 * RADIUS + 1, dtype=jnp.float32) - RADIUS
    raw_taps = jnp.exp(-offsets * offsets / (2.0 * sigma * sigma))
    return raw_taps / jnp.sum(raw_taps)


def band_matrix(weights, shift):
    inner = jnp.arange(BS, dtype=jnp.int32)
    lag = inner[:, None] + shift - inner[None, :]
    taps_index = jnp.arange(2 * RADIUS + 1, dtype=jnp.int32)
    picks = (lag[:, :, None] == taps_index[None, None, :]).astype(jnp.float32)
    return jnp.sum(picks * weights[None, None, :], axis=2)


def filter_first(extended, band_near, band_next):
    height, width = extended.shape
    block_count = (height - 2 * RADIUS) // BS
    padded = jnp.pad(extended, ((0, BS - 2 * RADIUS), (0, 0)))
    blocks = padded.reshape(block_count + 1, BS, width)
    result = jnp.einsum(
        "ij,bic->bjc", band_near, blocks[:block_count], precision=lax.Precision.HIGHEST
    )
    result = result + jnp.einsum(
        "ij,bic->bjc", band_next, blocks[1:], precision=lax.Precision.HIGHEST
    )
    return result.reshape(block_count * BS, width)


def filter_last(extended, band_near, band_next):
    height, width = extended.shape
    block_count = (width - 2 * RADIUS) // BS
    padded = jnp.pad(extended, ((0, 0), (0, BS - 2 * RADIUS)))
    blocks = padded.reshape(height, block_count + 1, BS)
    result = jnp.einsum(
        "mbi,ij->mbj", blocks[:, :block_count], band_near, precision=lax.Precision.HIGHEST
    )
    result = result + jnp.einsum(
        "mbi,ij->mbj", blocks[:, 1:], band_next, precision=lax.Precision.HIGHEST
    )
    return result.reshape(height, block_count * BS)


def per_device(density, design_mask, rebalance):
    tile_rows, tile_cols = density.shape
    weights = filter_taps()
    band_near = band_matrix(weights, 0)
    band_next = band_matrix(weights, BS)
    extended = with_halo(density, (("row", 0),), RADIUS)
    along_rows = filter_first(extended, band_near, band_next)
    widened = with_halo(along_rows, (("col", 1),), RADIUS)
    filtered = filter_last(widened, band_near, band_next)
    mask_rows, mask_cols = design_mask.shape
    cell_mask = jnp.broadcast_to(
        design_mask.astype(jnp.float32)[:, None, :, None], (mask_rows, BS, mask_cols, BS)
    )
    cell_mask = cell_mask.reshape(tile_rows, tile_cols)
    lower = jnp.tanh(SHARPNESS * THRESHOLD)
    upper = jnp.tanh(SHARPNESS * (1.0 - THRESHOLD))
    projected = cell_mask * (lower + jnp.tanh(SHARPNESS * (filtered - THRESHOLD))) / (lower + upper)
    total_volume = lax.psum(jnp.sum(projected), ("row", "col"))
    row_count = lax.axis_size("row")
    col_count = lax.axis_size("col")
    grid_cells = float(tile_rows * tile_cols * row_count * col_count)
    constraint = total_volume / grid_cells / VOLUME_TARGET - 1.0
    block_count = mask_rows * mask_cols
    device_count = row_count * col_count
    capacity = max(2, block_count // device_count)
    tiles = projected.astype(jnp.bfloat16).reshape(mask_rows, BS, mask_cols, BS)
    tiles = tiles.transpose(0, 2, 1, 3).reshape(block_count, BS * BS)
    local_index = jnp.arange(block_count, dtype=jnp.int32)
    block_row = lax.axis_index("row") * mask_rows + local_index // mask_cols
    block_col = lax.axis_index("col") * mask_cols + local_index % mask_cols
    global_id = block_row * (mask_cols * col_count) + block_col
    everywhere = jnp.arange(rebalance.shape[0], dtype=jnp.int32)
    matches = rebalance[None, :] == global_id[:, None]
    position = jnp.sum(jnp.where(matches, everywhere[None, :], 0), axis=1)
    target_dev = position // block_count
    target_slot = position % block_count
    earlier = (target_dev[:, None] == target_dev[None, :]) & (
        local_index[None, :] < local_index[:, None]
    )
    send_rank = jnp.sum(earlier.astype(jnp.int32), axis=1)
    send_row = target_dev * capacity + send_rank
    buffer_index = jnp.arange(device_count * capacity, dtype=jnp.int32)
    chosen = buffer_index[:, None] == send_row[None, :]
    outgoing = jnp.dot(
        chosen.astype(jnp.bfloat16), tiles, preferred_element_type=jnp.float32
    ).astype(jnp.bfloat16)
    out_slots = jnp.sum(jnp.where(chosen, target_slot[None, :] + 1, 0), axis=1) - 1
    flat_send = outgoing.reshape(device_count, capacity, BS * BS)
    flat_slots = out_slots.reshape(device_count, capacity)
    arrived, arrived_slots = (
        lax.all_to_all(flat_send, ("row", "col"), split_axis=0, concat_axis=0, tiled=True),
        lax.all_to_all(flat_slots, ("row", "col"), split_axis=0, concat_axis=0, tiled=True),
    )
    arrived = arrived.reshape(device_count * capacity, BS * BS)
    arrived_slots = arrived_slots.reshape(device_count * capacity)
    placing = (arrived_slots[None, :] == local_index[:, None]).astype(jnp.bfloat16)
    balanced = jnp.dot(placing, arrived, preferred_element_type=jnp.float32).astype(jnp.bfloat16)
    return (balanced.reshape(block_count, BS, BS), constraint)


def solution(mesh):
    return jax.shard_map(
        per_device,
        mesh=mesh,
        in_specs=(P("row", "col"), P("row", "col"), P()),
        out_specs=(P(("row", "col"), None, None), P()),
        check_vma=False,
    )
```

profile of v0, /device:TPU:0, one launch (start us, length us, event | category | flops | bytes accessed | tf_op | source)
XLA Modules:
  0.0 458.2 jit_solution(4022959359277284204)
XLA Ops:
  0.6 1.1 fusion.31
  1.7 2.4 collective-permute-start
  4.1 1.3 collective-permute-start.1
  5.4 0.6 fusion.29
  6.2 2.0 select_reduce_fusion
  8.5 0.7 broadcast_divide_fusion
  9.7 21.1 %pad_maximum_fusion = (f32[1024,4096]{1,0:T(8,128)}, f32[1024,4096]{1,0:T(8,128)}) fusion(f32[1024,4096]{1,0:T(8,128)} %param.3, f32[16,4096]{1,0:T(8,128)S(1)} %collective-permute-done, f32[16,4096]{1,0:T(8,128)S(1)} %collective-permute-done.1), kind=kLoop, calls=%fused_computation.12 | loop fusion | flops 33554432 | bytes 50855936 | tf_op jit(solution)/shard_map/concatenate | solution.py:24
  30.8 31.4 %fusion.16 = f32[8,4096,128]{1,2,0:T(8,128)} fusion(f32[8,128,4096]{2,1,0:T(8,128)} %bitcast.50, f32[128,128]{1,0:T(8,128)S(1)} %get-tuple-element.3), kind=kOutput, calls=%fused_computation.39 | convolution fusion | flops 6442450944 | bytes 33619968 | tf_op jit(solution)/shard_map/ij,bic->bjc/dot_general | solution.py:51
  62.2 24.2 %convolution_add_fusion = f32[8,4096,128]{1,2,0:T(8,128)} fusion(f32[8,4096,128]{1,2,0:T(8,128)} %fusion.16, f32[8,128,4096]{2,1,0:T(8,128)} %bitcast.52, f32[128,128]{1,0:T(8,128)S(1)} %get-tuple-element.2), kind=kOutput, calls=%fused_computation.18 | convolution fusion | flops 6446645248 | bytes 50397184 | tf_op jit(solution)/shard_map/ij,bic->bjc/dot_general | solution.py:48
  86.4 17.5 %copy.31 = f32[1024,4096]{0,1:T(8,128)} copy(f32[1024,4096]{1,0:T(8,128)} %bitcast.53) | data formatting | bytes 33554432 | tf_op jit(solution)/shard_map/reshape | solution.py:54
  103.9 0.9 fusion.30
  104.8 4.2 collective-permute-start.2
  109.0 1.3 collective-permute-start.3
  110.3 0.7 sub.66
  111.0 9.7 %all-to-all-start = ((s32[32,1,8]{2,1,0:T(1,128)}), s32[32,1,8]{2,1,0:T(1,128)S(1)}, u32[]{:S(2)}, u32[]{:S(2)}) async-start(s32[32,1,8]{2,1,0:T(1,128)} %bitcast), calls=%async_computation | async-start | bytes 32768 | tf_op jit(solution)/shard_map/all_to_all | solution.py:122
  120.9 7.0 %select_maximum_fusion = f32[1024,4224]{0,1:T(8,128)S(1)} fusion(f32[1024,16]{0,1:T(8,128)S(1)} %collective-permute-done.3, f32[1024,4096]{0,1:T(8,128)} %copy.31, f32[1024,16]{0,1:T(8,128)S(1)} %collective-permute-done.2), kind=kLoop, calls=%fused_computation.3 | loop fusion | flops 25952256 | bytes 34209792 | tf_op jit(solution)/shard_map/concatenate | solution.py:24
  128.0 29.6 %fusion.14 = f32[1024,32,128]{2,0,1:T(8,128)} fusion(f32[1024,33,128]{0,2,1:T(8,128)S(1)} %bitcast.48, f32[128,128]{1,0:T(8,128)S(1)} %get-tuple-element.3), kind=kOutput, calls=%fused_computation.37 | convolution fusion | flops 6442450944 | bytes 34144256 | tf_op jit(solution)/shard_map/mbi,ij->mbj/dot_general | solution.py:65
  157.6 39.0 %multiply_reduce_fusion = (f32[]{:T(128)}, f32[1024,32,128]{2,0,1:T(8,128)}) fusion(f32[1024,32]{0,1:T(8,128)S(1)} %bitcast.56, f32[1024,32,128]{2,0,1:T(8,128)} %fusion.14, f32[1024,33,128]{0,2,1:T(8,128)S(1)} %bitcast.49, f32[128,128]{1,0:T(8,128)S(1)} %get-tuple-element.2), kind=kOutput, calls=%fused_computation.16 | convolution fusion | flops 6471811072 | bytes 51052548 | tf_op jit(solution)/shard_map/mbi,ij->mbj/dot_general | solution.py:62
  196.6 6.9 %fusion.4 = bf16[8,128,32,128]{3,1,2,0:T(8,128)(2,1)S(1)} fusion(f32[8,128,32,128]{3,1,0,2:T(8,128)} %bitcast.51, f32[8,32]{1,0:T(8,128)S(1)} %convert_element_type.25), kind=kLoop, calls=%fused_computation.15 | loop fusion | flops 12582912 | bytes 25166848 | tf_op jit(solution)/shard_map/convert_element_type | solution.py:96
  203.5 20.7 %fusion = bf16[32,8,16384]{2,1,0:T(8,128)(2,1)} fusion(bf16[32,8,128,128]{3,2,1,0:T(8,128)(2,1)S(1)} %bitcast.54, s32[256]{0:T(256)S(1)} %multiply_add_fusion), kind=kOutput, calls=%fused_computation.2 | convolution fusion | flops 2151743488 | bytes 16778240 | tf_op jit(solution)/shard_map/dot_general | solution.py:114
  224.2 6.1 %all-to-all-start.1 = ((bf16[32,8,16384]{2,1,0:T(8,128)(2,1)}), bf16[32,8,16384]{2,1,0:T(8,128)(2,1)}, u32[]{:S(2)}, u32[]{:S(2)}) async-start(bf16[32,8,16384]{2,1,0:T(8,128)(2,1)} %fusion), calls=%async_computation.1 | async-start | bytes 16777216 | tf_op jit(solution)/shard_map/all_to_all | solution.py:121
  231.5 206.1 %psum.7 = f32[]{:T(128)} all-reduce(f32[]{:T(128)} %get-tuple-element.12), channel_id=1, replica_groups=mesh['row'=4,'col'=8] {'row','col'}, use_global_device_ids=true, to_apply=%region_7.8 | all-reduce | flops 1 | bytes 8 | tf_op jit(solution)/shard_map/psum | solution.py:88
  438.2 8.9 %fusion.8 = bf16[32,8,128,128]{3,1,2,0:T(8,128)(2,1)} fusion(bf16[32,8,16384]{2,1,0:T(8,128)(2,1)} %all-to-all-done.1, s32[256]{0:T(256)S(1)} %eq.95), kind=kOutput, calls=%fused_computation.23 | convolution fusion | flops 2151743488 | bytes 16778240 | tf_op jit(solution)/shard_map/dot_general | solution.py:127
  447.2 9.4 %copy.45 = bf16[32,8,128,128]{3,2,1,0:T(8,128)(2,1)} copy(bf16[32,8,128,128]{3,1,2,0:T(8,128)(2,1)} %fusion.8) | data formatting | bytes 16777216
  (24 shorter events, 2.3 us)
Async XLA Ops:
  1.7 8.0 %collective-permute-start = (f32[16,4096]{1,0:T(8,128)S(1)}, f32[16,4096]{1,0:T(8,128)S(1)}, u32[]{:S(2)}, u32[]{:S(2)}) collective-permute-start(f32[16,4096]{1,0:T(8,128)S(1)} %get-tuple-element.8), channel_id=1, source_target_pairs={{0,8},{8,16},{16,24},{1,9},{9,17},{17,25},{2,10},{10,18},{18,26},{... | collective-permute-start | bytes 786440 | tf_op jit(solution)/shard_map/ppermute | solution.py:22
  4.1 5.5 %collective-permute-start.1 = (f32[16,4096]{1,0:T(8,128)S(1)}, f32[16,4096]{1,0:T(8,128)S(1)}, u32[]{:S(2)}, u32[]{:S(2)}) collective-permute-start(f32[16,4096]{1,0:T(8,128)S(1)} %get-tuple-element.9), channel_id=1, source_target_pairs={{8,0},{16,8},{24,16},{9,1},{17,9},{25,17},{10,2},{18,10},{26,18},{... | collective-permute-start | bytes 786440 | tf_op jit(solution)/shard_map/ppermute | solution.py:23
  86.4 34.3 %copy-start = (s32[8,32]{1,0:T(8,128)S(1)}, s32[8,32]{1,0:T(8,128)}, u32[]{:S(2)}) copy-start(s32[8,32]{1,0:T(8,128)} %param.4) | copy-start | bytes 3076
  104.8 16.1 %collective-permute-start.2 = (f32[1024,16]{0,1:T(8,128)S(1)}, f32[1024,16]{0,1:T(8,128)S(1)}, u32[]{:S(2)}, u32[]{:S(2)}) collective-permute-start(f32[1024,16]{0,1:T(8,128)S(1)} %get-tuple-element.6), channel_id=1, source_target_pairs={{0,1},{1,2},{2,3},{3,4},{4,5},{5,6},{6,7},{8,9},{9,10},{10,11},{11... | collective-permute-start | bytes 196616 | tf_op jit(solution)/shard_map/ppermute | solution.py:22
  109.0 11.9 %collective-permute-start.3 = (f32[1024,16]{0,1:T(8,128)S(1)}, f32[1024,16]{0,1:T(8,128)S(1)}, u32[]{:S(2)}, u32[]{:S(2)}) collective-permute-start(f32[1024,16]{0,1:T(8,128)S(1)} %get-tuple-element.7), channel_id=1, source_target_pairs={{1,0},{2,1},{3,2},{4,3},{5,4},{6,5},{7,6},{9,8},{10,9},{11,10},{12... | collective-permute-start | bytes 196616 | tf_op jit(solution)/shard_map/ppermute | solution.py:23
  111.0 113.3 %all-to-all-start = ((s32[32,1,8]{2,1,0:T(1,128)}), s32[32,1,8]{2,1,0:T(1,128)S(1)}, u32[]{:S(2)}, u32[]{:S(2)}) async-start(s32[32,1,8]{2,1,0:T(1,128)} %bitcast), calls=%async_computation | async-start | bytes 32768 | tf_op jit(solution)/shard_map/all_to_all | solution.py:122
  224.2 214.0 %all-to-all-start.1 = ((bf16[32,8,16384]{2,1,0:T(8,128)(2,1)}), bf16[32,8,16384]{2,1,0:T(8,128)(2,1)}, u32[]{:S(2)}, u32[]{:S(2)}) async-start(bf16[32,8,16384]{2,1,0:T(8,128)(2,1)} %fusion), calls=%async_computation.1 | async-start | bytes 16777216 | tf_op jit(solution)/shard_map/all_to_all | solution.py:121
where the time goes:
time: 467 us; the launch traced here: 458 us
  blocking collectives  206 us (44%)
  matrix products  154 us (33%)
  other arithmetic  39.9 us (9%)
  local copies, waits for them, and re-layouts  30.2 us (6%)
  starting transfers between devices  25 us (5%)
    psum x1, blocking collectives, per_device(): total_volume = lax.psum(jnp.sum(projected), ('row', 'col'))  206 us
    dot_general x1, matrix products, filter_last(): jnp.einsum('mbi,ij->mbj', blocks[:, :block_count], band_near, precision=l...  39 us
    dot_general x1, matrix products, filter_first(): jnp.einsum('ij,bic->bjc', band_next, blocks[1:], precision=lax.Precision....  31.4 us
    dot_general x1, matrix products, filter_last(): jnp.einsum('mbi,ij->mbj', blocks[:, 1:], band_next, precision=lax.Precisi...  29.6 us
    concatenate x2, other arithmetic, with_halo(): shard = jnp.concatenate([before, shard, after], axis=dim)  28.2 us
    dot_general x1, matrix products, filter_first(): jnp.einsum('ij,bic->bjc', band_near, blocks[:block_count], precision=lax....  24.2 us
    dot_general x1, matrix products, per_device(): jnp.dot(chosen.astype(jnp.bfloat16), tiles, preferred_element_type=jnp.fl...  20.7 us
    reshape x1, local copies, waits for them, and re-layouts, filter_first(): return result.reshape(block_count * BS, width)  17.5 us
  transfers between devices with their start and end apart: 6, of which 0 were waited for; matrix products, arithmetic and copies ran while one was open for 24% of the time, Pallas kernels for 0%

commit v1 on v0

v1 whole, which is shorter than its diff:
```python
import functools

import jax
import jax.numpy as jnp
import numpy as np
from jax import lax
from jax.experimental import pallas as pl
from jax.experimental.pallas import tpu as pltpu
from jax.sharding import PartitionSpec as P

BS = 128
RADIUS = 16
SHARPNESS = 32.0
THRESHOLD = 0.5
VOLUME_TARGET = 0.4
MESH = pl.DeviceIdType.MESH
MIB = 2**20


def filter_taps():
    sigma = RADIUS / 4.0
    offsets = np.arange(2 * RADIUS + 1, dtype=np.float64) - RADIUS
    raw_taps = np.exp(-offsets * offsets / (2.0 * sigma * sigma))
    return (raw_taps / raw_taps.sum()).astype(np.float32)


def split(x):
    high = x.astype(jnp.bfloat16)
    return high, (x - high.astype(jnp.float32)).astype(jnp.bfloat16)


def bands():
    taps = filter_taps()
    rows = np.zeros((BS, BS + 2 * RADIUS), np.float32)
    cols = np.zeros((2 * BS, BS), np.float32)
    for out in range(BS):
        for e in range(2 * RADIUS + 1):
            rows[out, out + e] = taps[e]
            source = out + e - RADIUS
            at = source if 0 <= source < BS else BS + source % BS
            cols[at, out] = taps[e]
    return split(jnp.asarray(rows)) + split(jnp.asarray(cols))


def project_block(field, row, col, mask, row_high, row_low, col_high, col_low):
    top = pl.multiple_of(row * BS, BS)
    left = pl.multiple_of(col * BS, BS)
    rows = pl.ds(top, BS + 2 * RADIUS)
    before = field[rows, pl.ds(left, BS)]
    own = field[rows, pl.ds(pl.multiple_of(left + BS, BS), BS)]
    after = field[rows, pl.ds(pl.multiple_of(left + 2 * BS, BS), BS)]
    lane = lax.broadcasted_iota(jnp.int32, own.shape, 1)
    side = jnp.where(lane < BS // 2, after, before)
    high, low = split(jnp.concatenate([own, side], axis=1))
    dot = functools.partial(jnp.dot, preferred_element_type=jnp.float32)
    along = dot(high, col_high[...]) + (dot(low, col_high[...]) + dot(high, col_low[...]))
    high, low = split(along)
    filtered = dot(row_high[...], high) + (dot(row_high[...], low) + dot(row_low[...], high))
    lower = float(np.tanh(np.float32(SHARPNESS * THRESHOLD)))
    upper = float(np.tanh(np.float32(SHARPNESS * (1.0 - THRESHOLD))))
    return (lower + jnp.tanh(SHARPNESS * (filtered - THRESHOLD))) * (mask.astype(jnp.float32) / (lower + upper))


def load_field(field, density, top, bottom, left, right, sem):
    height, width = density.shape
    full = height + 2 * RADIUS
    copies = [
        pltpu.make_async_copy(density, field.at[pl.ds(RADIUS, height), pl.ds(BS, width)], sem.at[0]),
        pltpu.make_async_copy(top, field.at[pl.ds(0, RADIUS), pl.ds(BS, width)], sem.at[1]),
        pltpu.make_async_copy(bottom, field.at[pl.ds(RADIUS + height, RADIUS), pl.ds(BS, width)], sem.at[2]),
        pltpu.make_async_copy(left, field.at[pl.ds(0, full), pl.ds(0, BS)], sem.at[3]),
        pltpu.make_async_copy(right, field.at[pl.ds(0, full), pl.ds(BS + width, BS)], sem.at[4]),
    ]
    for copy in copies:
        copy.start()
    for copy in copies:
        copy.wait()


def halos(density):
    def shift(x, axis, step):
        n = lax.axis_size(axis)
        return lax.ppermute(x, axis, [(i, i + step) for i in range(n) if 0 <= i + step < n])

    top = shift(density[-RADIUS:], "row", 1)
    bottom = shift(density[:RADIUS], "row", -1)
    edges = [
        jnp.concatenate([top[:, cut], density[:, cut], bottom[:, cut]], axis=0)
        for cut in (slice(-RADIUS, None), slice(0, RADIUS))
    ]
    left = jnp.pad(shift(edges[0], "col", 1), ((0, 0), (BS - RADIUS, 0)))
    right = jnp.pad(shift(edges[1], "col", -1), ((0, 0), (0, BS - RADIUS)))
    return top, bottom, left, right


def routing(rebalance, mask_rows, mask_cols, capacity):
    row_count, col_count = lax.axis_size("row"), lax.axis_size("col")
    devices, count = row_count * col_count, mask_rows * mask_cols
    me = lax.axis_index("row") * col_count + lax.axis_index("col")
    wanted = rebalance.reshape(devices, count)
    block_row, block_col = wanted // (mask_cols * col_count), wanted % (mask_cols * col_count)
    source = (block_row // mask_rows) * col_count + block_col // mask_cols
    local = (block_row % mask_rows) * mask_cols + block_col % mask_cols
    slot = jnp.arange(count, dtype=jnp.int32)
    upto = (slot[:, None] <= slot[None, :]).astype(jnp.bfloat16)
    mine = source == me
    seen = jnp.dot(mine.astype(jnp.bfloat16), upto, preferred_element_type=jnp.float32).astype(jnp.int32)
    order = jnp.stack(
        [jnp.sum(jnp.where(mine & (seen == k + 1), local, 0), axis=1) for k in range(capacity)], axis=1
    )
    here = lax.dynamic_slice_in_dim(source, me, 1, axis=0)
    from_each = here == jnp.arange(devices, dtype=jnp.int32)[:, None]
    arrived = jnp.dot(from_each.astype(jnp.bfloat16), upto, preferred_element_type=jnp.float32).astype(jnp.int32)
    slots = jnp.stack(
        [jnp.sum(jnp.where(from_each & (arrived == k + 1), slot[None, :], 0), axis=1) for k in range(capacity)], axis=1
    )
    return order, slots


def place_kernel(groups, slots, arrived, *rest):
    out, held, load_sem, store_sem = rest[-4:]
    size = held.shape[1]

    def load(g):
        return pltpu.make_async_copy(arrived.at[pl.ds(g * size, size)], held.at[g], load_sem.at[g])

    for g in range(groups):
        load(g).start()
    for g in range(groups):
        load(g).wait()
        for i in range(size):
            pltpu.make_async_copy(held.at[g, i], out.at[slots[g * size + i]], store_sem.at[g]).start()
    for g in range(groups):
        pltpu.make_async_copy(held.at[g], out.at[pl.ds(g * size, size)], store_sem.at[g]).wait()


def place(arrived, slots, count, before=None):
    total = arrived.shape[0]
    size = max(s for s in (16, 8, 4, 2, 1) if total % s == 0)
    groups = total // size
    any_space = pl.BlockSpec(memory_space=pl.ANY)
    args = (slots, arrived) + (() if before is None else (before,))
    return pl.pallas_call(
        functools.partial(place_kernel, groups),
        out_shape=jax.ShapeDtypeStruct((count, BS, BS), jnp.bfloat16),
        in_specs=[pl.BlockSpec(memory_space=pltpu.SMEM)] + [any_space] * (len(args) - 1),
        out_specs=any_space,
        scratch_shapes=[
            pltpu.VMEM((groups, size, BS, BS), jnp.bfloat16),
            pltpu.SemaphoreType.DMA((groups,)),
            pltpu.SemaphoreType.DMA((groups,)),
        ],
        input_output_aliases={} if before is None else {2: 0},
        compiler_params=pltpu.CompilerParams(vmem_limit_bytes=24 * MIB),
        cost_estimate=pl.CostEstimate(flops=0, bytes_accessed=2 * arrived.size * 2, transcendentals=0),
        name="place",
    )(*args)


def project_kernel(mask_cols, order, mask, density, top, bottom, left, right, rh, rl, ch, cl, out, total, field, sem):
    @pl.when(pl.program_id(0) == 0)
    def _():
        load_field(field, density, top, bottom, left, right, sem)
        total[...] = jnp.zeros_like(total)

    size = out.shape[0]
    base = pl.program_id(0) * size

    @pl.loop(0, size)
    def _(i):
        block = order[base + i]
        cells = project_block(field, block // mask_cols, block % mask_cols, mask[block], rh, rl, ch, cl)
        total[...] += cells
        out[i] = cells.astype(jnp.bfloat16)


def project(order, mask, mask_cols, density, sides, band):
    count = order.shape[0]
    size = max(s for s in (16, 8, 4, 2, 1) if count % s == 0)
    height, width = density.shape
    any_space = pl.BlockSpec(memory_space=pl.ANY)
    whole = pl.BlockSpec(memory_space=pltpu.VMEM)
    scalar = pl.BlockSpec(memory_space=pltpu.SMEM)
    return pl.pallas_call(
        functools.partial(project_kernel, mask_cols),
        grid=(count // size,),
        out_shape=(
            jax.ShapeDtypeStruct((count, BS, BS), jnp.bfloat16),
            jax.ShapeDtypeStruct((BS, BS), jnp.float32),
        ),
        in_specs=[scalar] * 2 + [any_space] * 5 + [whole] * 4,
        out_specs=(pl.BlockSpec((size, BS, BS), lambda i: (i, 0, 0)), pl.BlockSpec((BS, BS), lambda i: (0, 0))),
        scratch_shapes=[
            pltpu.VMEM((height + 2 * RADIUS, width + 2 * BS), jnp.float32),
            pltpu.SemaphoreType.DMA((5,)),
        ],
        compiler_params=pltpu.CompilerParams(vmem_limit_bytes=40 * MIB, dimension_semantics=("arbitrary",)),
        cost_estimate=pl.CostEstimate(flops=count * BS * BS * 2000, bytes_accessed=density.size * 4, transcendentals=count * BS * BS),
        name="project",
    )(order, mask, density, *sides, *band)


def per_device(density, design_mask, rebalance):
    mask_rows, mask_cols = design_mask.shape
    count = mask_rows * mask_cols
    row_count, col_count = lax.axis_size("row"), lax.axis_size("col")
    devices = row_count * col_count
    capacity = count // devices
    order, slots = routing(rebalance, mask_rows, mask_cols, capacity)
    sides = halos(density)
    mask = design_mask.reshape(count)
    band = bands()
    cuts = sorted({0, max(1, capacity // 8), max(1, capacity // 2), capacity})
    balanced, volume = None, 0.0
    for a, b in zip(cuts[:-1], cuts[1:]):
        blocks, cells = project(order[:, a:b].reshape(-1), mask, mask_cols, density, sides, band)
        volume = volume + cells
        arrived = lax.all_to_all(
            blocks.reshape(devices, b - a, BS, BS), ("row", "col"), split_axis=0, concat_axis=0, tiled=True
        )
        balanced = place(arrived.reshape(-1, BS, BS), slots[:, a:b].reshape(-1), count, balanced)
    total_volume = lax.psum(jnp.sum(volume), ("row", "col"))
    constraint = total_volume / float(density.size * devices) / VOLUME_TARGET - 1.0
    return balanced, constraint


def solution(mesh):
    return jax.shard_map(
        per_device,
        mesh=mesh,
        in_specs=(P("row", "col"), P("row", "col"), P()),
        out_specs=(P(("row", "col"), None, None), P()),
        check_vma=False,
    )
```

time: 467 us -> 316 us (0.68); the launches traced: 458 us -> 315 us
  matrix products: 154 us -> 1.36 us
  Pallas kernels: 0 us -> 142 us
  blocking collectives: 206 us -> 112 us
  other arithmetic: 39.9 us -> 2.03 us
  local copies, waits for them, and re-layouts: 30.2 us -> 21.9 us
  starting transfers between devices: 25 us -> 32.1 us
    dot_general x6 -> x2, matrix products: 154 us -> 1.36 us  [the longest x1 0.98 us: routing(): jnp.dot(mine.astype(jnp.bfloat16), upto, preferred_element_type=jnp.float32)]
    pallas_call x0 -> x6, Pallas kernels: none -> 142 us  [the longest x3 134 us: project(): pl.pallas_call(functools.partial(project_kernel, mask_cols), grid=(count...]
    psum x1, blocking collectives: 206 us -> 112 us  [per_device(): total_volume = lax.psum(jnp.sum(volume), ('row', 'col'))]
    concatenate x2 -> x0, other arithmetic: 28.2 us -> none  [with_halo(): shard = jnp.concatenate([before, shard, after], axis=dim)]
    reshape x1 -> x6, local copies, waits for them, and re-layouts: 17.5 us -> 2.67 us  [the longest x2 0.92 us: per_device(): order[:, a:b].reshape(-1)]
    convert_element_type x2 -> x0, other arithmetic: 6.91 us -> none  [the longest x1 6.91 us: per_device(): tiles = projected.astype(jnp.bfloat16).reshape(mask_rows, BS, mask_cols, BS)]
    all_to_all x2 -> x3, starting transfers between devices: 15.8 us -> 22.4 us  [per_device(): lax.all_to_all(blocks.reshape(devices, b - a, BS, BS), ('row', 'col'), sp...]
    unnamed x4 -> x48, local copies, waits for them, and re-layouts: 9.39 us -> 13.8 us
  transfers between devices with their start and end apart: 6 -> 7, of which waited for: 0 -> 2; matrix products, arithmetic and copies ran while one was open for 24% -> 3% of each run, Pallas kernels for 0% -> 37%
where the time goes in v1:
time: 316 us; the launch traced here: 315 us
  Pallas kernels  142 us (45%)
  blocking collectives  112 us (35%)
  starting transfers between devices  32.1 us (10%)
  local copies, waits for them, and re-layouts  21.9 us (7%)
    pallas_call x3, Pallas kernels, project(): pl.pallas_call(functools.partial(project_kernel, mask_cols), grid=(count...  134 us
    psum x1, blocking collectives, per_device(): total_volume = lax.psum(jnp.sum(volume), ('row', 'col'))  112 us
    all_to_all x3, starting transfers between devices, per_device(): lax.all_to_all(blocks.reshape(devices, b - a, BS, BS), ('row', 'col'), sp...  22.4 us
    unnamed x48, local copies, waits for them, and re-layouts  13.8 us
    ppermute x4, starting transfers between devices, shift(): lax.ppermute(x, axis, [(i, i + step) for i in range(n) if 0 <= i + step <...  9.74 us
    pallas_call x3, Pallas kernels, place(): pl.pallas_call(functools.partial(place_kernel, groups), out_shape=jax.Sha...  8.18 us
  transfers between devices with their start and end apart: 7, of which 2 were waited for; matrix products, arithmetic and copies ran while one was open for 3% of the time, Pallas kernels for 37%

profile of v1, /device:TPU:0, one launch (start us, length us, event | category | flops | bytes accessed | tf_op | source)
XLA Modules:
  0.0 315.1 jit_solution(6927018710614654267)
XLA Ops:
  0.7 1.1 fusion.21
  1.8 2.4 collective-permute-start
  4.2 1.3 collective-permute-start.1
  5.5 1.4 fusion.20
  10.0 1.3 collective-permute-start.3
  11.6 4.7 %collective-permute-start.2 = (f32[1056,16]{0,1:T(8,128)S(1)}, f32[1056,16]{0,1:T(8,128)S(1)}, u32[]{:S(2)}, u32[]{:S(2)}) collective-permute-start(f32[1056,16]{0,1:T(8,128)S(1)} %concatenate.10), channel_id=1, source_target_pairs={{0,1},{1,2},{2,3},{3,4},{4,5},{5,6},{6,7},{8,9},{9,10},{10,11},{11... | collective-permute-start | bytes 202760 | tf_op jit(solution)/shard_map/ppermute | solution.py:83
  16.3 1.0 select_reduce_fusion
  18.8 20.8 %project.5 = (bf16[32,128,128]{2,1,0:T(8,128)(2,1)S(1)}, f32[128,128]{1,0:T(8,128)S(1)}) custom-call(s32[32]{0:T(128)S(1)} %get-tuple-element.14.order, s32[256]{0:T(256)S(1)} %reshape.43.mask, f32[1024,4096]{1,0:T(8,128)} %density.5, f32[16,4096]{1,0:T(8,128)S(1)} %collective-permute-done.top, f32[16,4096]{1,0:T(8,128)S(1)} %collective-permute-done.1.bottom, ...), custom_call_target="tpu_custom_call" | custom-call | flops 1048576000 | bytes 16777216 | tf_op jit(solution)/shard_map/project/pallas_call | solution.py:184
  39.5 1.0 copy-done.10
  41.1 10.6 %all-to-all-start.2 = ((bf16[32,1,128,128]{3,2,1,0:T(8,128)(2,1)}), bf16[32,1,128,128]{3,2,1,0:T(8,128)(2,1)S(1)}, u32[]{:S(2)}, u32[]{:S(2)}) async-start(bf16[32,1,128,128]{3,2,1,0:T(8,128)(2,1)} %bitcast.28), calls=%async_computation.2 | async-start | bytes 2097152 | tf_op jit(solution)/shard_map/all_to_all | solution.py:218
  52.0 49.5 %project.4 = (bf16[96,128,128]{2,1,0:T(8,128)(2,1)S(1)}, f32[128,128]{1,0:T(8,128)S(1)}) custom-call(s32[96]{0:T(128)S(1)} %reshape.47.order, s32[256]{0:T(256)S(1)} %reshape.43.mask, f32[1024,4096]{1,0:T(8,128)} %density.5, f32[16,4096]{1,0:T(8,128)S(1)} %collective-permute-done.top, f32[16,4096]{1,0:T(8,128)S(1)} %collective-permute-done.1.bottom, ...), custom_call_target="tpu_custom_call" | custom-call | flops 3145728000 | bytes 16777216 | tf_op jit(solution)/shard_map/project/pallas_call | solution.py:184
  101.5 1.7 copy-done.7
  103.8 1.1 copy-done.4
  104.8 5.8 %all-to-all-start.1 = ((bf16[32,3,128,128]{3,2,1,0:T(8,128)(2,1)}), bf16[32,3,128,128]{3,2,1,0:T(8,128)(2,1)S(1)}, u32[]{:S(2)}, u32[]{:S(2)}) async-start(bf16[32,3,128,128]{3,2,1,0:T(8,128)(2,1)} %bitcast.27), calls=%async_computation.1 | async-start | bytes 6291456 | tf_op jit(solution)/shard_map/all_to_all | solution.py:218
  112.9 1.0 copy-done.1
  113.9 1.0 copy-done.3
  117.6 63.9 %project.3 = (bf16[128,128,128]{2,1,0:T(8,128)(2,1)S(1)}, f32[128,128]{1,0:T(8,128)S(1)}) custom-call(s32[128]{0:T(128)S(1)} %reshape.42.order, s32[256]{0:T(256)S(1)} %reshape.43.mask, f32[1024,4096]{1,0:T(8,128)} %density.5, f32[16,4096]{1,0:T(8,128)S(1)} %collective-permute-done.top, f32[16,4096]{1,0:T(8,128)S(1)} %copy-done.9, ...), custom_call_target="tpu_custom_call" | custom-call | flops 4194304000 | bytes 16777216 | tf_op jit(solution)/shard_map/project/pallas_call | solution.py:184
  181.5 1.9 copy-done.6
  184.0 6.0 %all-to-all-start = ((bf16[32,4,128,128]{3,2,1,0:T(8,128)(2,1)}), bf16[32,4,128,128]{3,2,1,0:T(8,128)(2,1)}, u32[]{:S(2)}, u32[]{:S(2)}) async-start(bf16[32,4,128,128]{3,2,1,0:T(8,128)(2,1)} %bitcast.26), calls=%async_computation | async-start | bytes 8388608 | tf_op jit(solution)/shard_map/all_to_all | solution.py:218
  192.1 111.8 %psum.7 = f32[]{:T(128)} all-reduce(f32[]{:T(128)} %add_reduce_fusion), channel_id=1, replica_groups=mesh['row'=4,'col'=8] {'row','col'}, use_global_device_ids=true, to_apply=%region_17.18 | all-reduce | flops 1 | bytes 8 | tf_op jit(solution)/shard_map/psum | solution.py:222
  304.6 1.2 copy-done.5
  305.8 1.6 place.3.rest_0_
  307.4 2.5 place.4.rest_0_
  309.9 4.1 %place.5 = bf16[256,128,128]{2,1,0:T(8,128)(2,1)} custom-call(s32[128]{0:T(128)S(1)} %reshape.41.slots, bf16[128,128,128]{2,1,0:T(8,128)(2,1)} %bitcast.10.arrived, bf16[256,128,128]{2,1,0:T(8,128)(2,1)} %place.4.rest_0_), custom_call_target="tpu_custom_call", output_to_operand_aliasing={{}: (2, {})} | custom-call | bytes 8388608 | tf_op jit(solution)/shard_map/place/pallas_call | solution.py:143
  (78 shorter events, 13.7 us)
Async XLA Ops:
  0.6 18.1 %copy-start.11 = (bf16[128,160]{1,0:T(8,128)(2,1)S(1)}, bf16[128,160]{1,0:T(8,128)(2,1)}, u32[]{:S(2)}) copy-start(bf16[128,160]{1,0:T(8,128)(2,1)} %constant.110.rh) | copy-start | bytes 122884
  0.6 18.1 %copy-start.12 = (bf16[128,160]{1,0:T(8,128)(2,1)S(1)}, bf16[128,160]{1,0:T(8,128)(2,1)}, u32[]{:S(2)}) copy-start(bf16[128,160]{1,0:T(8,128)(2,1)} %constant.113.rl) | copy-start | bytes 122884
  0.7 18.1 %copy-start.13 = (bf16[256,128]{1,0:T(8,128)(2,1)S(1)}, bf16[256,128]{1,0:T(8,128)(2,1)}, u32[]{:S(2)}) copy-start(bf16[256,128]{1,0:T(8,128)(2,1)} %constant.114.ch) | copy-start | bytes 196612
  0.7 18.1 %copy-start.15 = (bf16[256,128]{1,0:T(8,128)(2,1)S(1)}, bf16[256,128]{1,0:T(8,128)(2,1)}, u32[]{:S(2)}) copy-start(bf16[256,128]{1,0:T(8,128)(2,1)} %constant.117.cl) | copy-start | bytes 196612
  1.8 7.7 %collective-permute-start = (f32[16,4096]{1,0:T(8,128)S(1)}, f32[16,4096]{1,0:T(8,128)S(1)}, u32[]{:S(2)}, u32[]{:S(2)}) collective-permute-start(f32[16,4096]{1,0:T(8,128)S(1)} %get-tuple-element.35), channel_id=1, source_target_pairs={{0,8},{8,16},{16,24},{1,9},{9,17},{17,25},{2,10},{10,18},{18,26},{... | collective-permute-start | bytes 786440 | tf_op jit(solution)/shard_map/ppermute | solution.py:83
  4.2 5.5 %collective-permute-start.1 = (f32[16,4096]{1,0:T(8,128)S(1)}, f32[16,4096]{1,0:T(8,128)S(1)}, u32[]{:S(2)}, u32[]{:S(2)}) collective-permute-start(f32[16,4096]{1,0:T(8,128)S(1)} %get-tuple-element.34), channel_id=1, source_target_pairs={{8,0},{16,8},{24,16},{9,1},{17,9},{25,17},{10,2},{18,10},{26,18},{... | collective-permute-start | bytes 786440 | tf_op jit(solution)/shard_map/ppermute | solution.py:83
  9.8 42.2 %copy-start.8 = (f32[16,4096]{1,0:T(8,128)}, f32[16,4096]{1,0:T(8,128)S(1)}, u32[]{:S(2)}) copy-start(f32[16,4096]{1,0:T(8,128)S(1)} %collective-permute-done.1.bottom) | copy-start | bytes 786436
  10.0 7.3 %collective-permute-start.3 = (f32[1056,16]{0,1:T(8,128)S(1)}, f32[1056,16]{0,1:T(8,128)S(1)}, u32[]{:S(2)}, u32[]{:S(2)}) collective-permute-start(f32[1056,16]{0,1:T(8,128)S(1)} %concatenate.11), channel_id=1, source_target_pairs={{1,0},{2,1},{3,2},{4,3},{5,4},{6,5},{7,6},{9,8},{10,9},{11,10},{12... | collective-permute-start | bytes 202760 | tf_op jit(solution)/shard_map/ppermute | solution.py:83
  11.6 6.7 %collective-permute-start.2 = (f32[1056,16]{0,1:T(8,128)S(1)}, f32[1056,16]{0,1:T(8,128)S(1)}, u32[]{:S(2)}, u32[]{:S(2)}) collective-permute-start(f32[1056,16]{0,1:T(8,128)S(1)} %concatenate.10), channel_id=1, source_target_pairs={{0,1},{1,2},{2,3},{3,4},{4,5},{5,6},{6,7},{8,9},{9,10},{10,11},{11... | collective-permute-start | bytes 202760 | tf_op jit(solution)/shard_map/ppermute | solution.py:83
  17.6 34.4 %copy-start = (f32[1056,128]{1,0:T(8,128)}, f32[1056,128]{1,0:T(8,128)S(1)}, u32[]{:S(2)}) copy-start(f32[1056,128]{1,0:T(8,128)S(1)} %pad.9.right) | copy-start | bytes 1622020
  18.7 33.2 %copy-start.2 = (f32[1056,128]{1,0:T(8,128)}, f32[1056,128]{1,0:T(8,128)S(1)}, u32[]{:S(2)}) copy-start(f32[1056,128]{1,0:T(8,128)S(1)} %pad.8.left) | copy-start | bytes 1622020
  39.5 1.0 copy-start.10
  41.1 62.6 %all-to-all-start.2 = ((bf16[32,1,128,128]{3,2,1,0:T(8,128)(2,1)}), bf16[32,1,128,128]{3,2,1,0:T(8,128)(2,1)S(1)}, u32[]{:S(2)}, u32[]{:S(2)}) async-start(bf16[32,1,128,128]{3,2,1,0:T(8,128)(2,1)} %bitcast.28), calls=%async_computation.2 | async-start | bytes 2097152 | tf_op jit(solution)/shard_map/all_to_all | solution.py:218
  101.5 1.7 copy-start.7
  103.8 1.1 copy-start.4
  104.8 79.2 %all-to-all-start.1 = ((bf16[32,3,128,128]{3,2,1,0:T(8,128)(2,1)}), bf16[32,3,128,128]{3,2,1,0:T(8,128)(2,1)S(1)}, u32[]{:S(2)}, u32[]{:S(2)}) async-start(bf16[32,3,128,128]{3,2,1,0:T(8,128)(2,1)} %bitcast.27), calls=%async_computation.1 | async-start | bytes 6291456 | tf_op jit(solution)/shard_map/all_to_all | solution.py:218
  112.9 1.1 copy-start.1
  113.9 1.0 copy-start.3
  181.5 1.9 copy-start.6
  184.0 7.4 %copy-start.18 = (f32[128,128]{1,0:T(8,128)S(1)}, f32[128,128]{1,0:T(8,128)}, u32[]{:S(2)}) copy-start(f32[128,128]{1,0:T(8,128)} %copy-done.17) | copy-start | bytes 196612
  184.0 7.4 %copy-start.20 = (f32[128,128]{1,0:T(8,128)S(1)}, f32[128,128]{1,0:T(8,128)}, u32[]{:S(2)}) copy-start(f32[128,128]{1,0:T(8,128)} %copy-done.19) | copy-start | bytes 196612
  184.0 7.4 %copy-start.22 = (f32[128,128]{1,0:T(8,128)S(1)}, f32[128,128]{1,0:T(8,128)}, u32[]{:S(2)}) copy-start(f32[128,128]{1,0:T(8,128)} %copy-done.21) | copy-start | bytes 196612
  184.0 125.8 %all-to-all-start = ((bf16[32,4,128,128]{3,2,1,0:T(8,128)(2,1)}), bf16[32,4,128,128]{3,2,1,0:T(8,128)(2,1)}, u32[]{:S(2)}, u32[]{:S(2)}) async-start(bf16[32,4,128,128]{3,2,1,0:T(8,128)(2,1)} %bitcast.26), calls=%async_computation | async-start | bytes 8388608 | tf_op jit(solution)/shard_map/all_to_all | solution.py:218
  304.6 1.2 copy-start.5
  (6 other events, 4.5 us)

commit v2 on v1

--- a/solution.py
+++ b/solution.py
@@ -42,13 +42,7 @@
     return split(jnp.asarray(rows)) + split(jnp.asarray(cols))
 
 
-def project_block(field, row, col, mask, row_high, row_low, col_high, col_low):
-    top = pl.multiple_of(row * BS, BS)
-    left = pl.multiple_of(col * BS, BS)
-    rows = pl.ds(top, BS + 2 * RADIUS)
-    before = field[rows, pl.ds(left, BS)]
-    own = field[rows, pl.ds(pl.multiple_of(left + BS, BS), BS)]
-    after = field[rows, pl.ds(pl.multiple_of(left + 2 * BS, BS), BS)]
+def project_block(before, own, after, mask, row_high, row_low, col_high, col_low):
     lane = lax.broadcasted_iota(jnp.int32, own.shape, 1)
     side = jnp.where(lane < BS // 2, after, before)
     high, low = split(jnp.concatenate([own, side], axis=1))
@@ -61,19 +55,34 @@
     return (lower + jnp.tanh(SHARPNESS * (filtered - THRESHOLD))) * (mask.astype(jnp.float32) / (lower + upper))
 
 
-def load_field(field, density, top, bottom, left, right, sem):
-    height, width = density.shape
-    full = height + 2 * RADIUS
-    copies = [
-        pltpu.make_async_copy(density, field.at[pl.ds(RADIUS, height), pl.ds(BS, width)], sem.at[0]),
-        pltpu.make_async_copy(top, field.at[pl.ds(0, RADIUS), pl.ds(BS, width)], sem.at[1]),
-        pltpu.make_async_copy(bottom, field.at[pl.ds(RADIUS + height, RADIUS), pl.ds(BS, width)], sem.at[2]),
-        pltpu.make_async_copy(left, field.at[pl.ds(0, full), pl.ds(0, BS)], sem.at[3]),
-        pltpu.make_async_copy(right, field.at[pl.ds(0, full), pl.ds(BS + width, BS)], sem.at[4]),
-    ]
-    for copy in copies:
+def load_tiles(tiles, density, top, bottom, left, right, sem):
+    height = density.shape[0]
+    mask_cols, mask_rows = tiles.shape[0] - 2, tiles.shape[1]
+    waits = []
+
+    def begin(source, goal, at):
+        copy = pltpu.make_async_copy(source, goal, sem.at[at])
         copy.start()
-    for copy in copies:
+        waits.append(copy)
+
+    for r in range(mask_rows):
+        low, high = max(r * BS - RADIUS, 0), min((r + 1) * BS + RADIUS, height)
+        inside = pl.ds(low - (r * BS - RADIUS), high - low)
+
+        @pl.loop(0, mask_cols)
+        def _(c):
+            cut = density.at[pl.ds(low, high - low), pl.ds(pl.multiple_of(c * BS, BS), BS)]
+            pltpu.make_async_copy(cut, tiles.at[c + 1, r, inside], sem.at[r]).start()
+
+        loaded = tiles.at[pl.ds(1, mask_cols), r, inside]
+        waits.append(pltpu.make_async_copy(loaded, loaded, sem.at[r]))
+        window = pl.ds(r * BS, BS + 2 * RADIUS)
+        begin(left.at[window], tiles.at[0, r], mask_rows + r)
+        begin(right.at[window], tiles.at[mask_cols + 1, r], 2 * mask_rows + r)
+    inner = pl.ds(1, mask_cols)
+    begin(top, tiles.at[inner, 0, pl.ds(0, RADIUS)], 3 * mask_rows)
+    begin(bottom, tiles.at[inner, mask_rows - 1, pl.ds(BS + RADIUS, RADIUS)], 3 * mask_rows + 1)
+    for copy in waits:
         copy.wait()
 
 
@@ -90,7 +99,8 @@
     ]
     left = jnp.pad(shift(edges[0], "col", 1), ((0, 0), (BS - RADIUS, 0)))
     right = jnp.pad(shift(edges[1], "col", -1), ((0, 0), (0, BS - RADIUS)))
-    return top, bottom, left, right
+    strips = [x.reshape(RADIUS, -1, BS).transpose(1, 0, 2) for x in (top, bottom)]
+    return (*strips, left, right)
 
 
 def routing(rebalance, mask_rows, mask_cols, capacity):
@@ -157,70 +167,145 @@
     )(*args)
 
 
-def project_kernel(mask_cols, order, mask, density, top, bottom, left, right, rh, rl, ch, cl, out, total, field, sem):
-    @pl.when(pl.program_id(0) == 0)
-    def _():
-        load_field(field, density, top, bottom, left, right, sem)
-        total[...] = jnp.zeros_like(total)
-
-    size = out.shape[0]
-    base = pl.program_id(0) * size
-
-    @pl.loop(0, size)
-    def _(i):
-        block = order[base + i]
-        cells = project_block(field, block // mask_cols, block % mask_cols, mask[block], rh, rl, ch, cl)
+def exchange_kernel(
+    sizes, block_row, block_col, mask, density, top, bottom, left, right, rh, rl, ch, cl,
+    arrived, volume, tiles, outgoing, total, sums, load_sem, send_sem, recv_sem, sum_send, sum_recv,
+):
+    row_count, col_count = sizes
+    devices, capacity = outgoing.shape[:2]
+    row, col = lax.axis_index("row"), lax.axis_index("col")
+    me = row * col_count + col
+    half, quarter = col_count // 2, col_count // 4
+    near = quarter * row_count
+
+    def place_of(device):
+        return (device // col_count, device % col_count)
+
+    def target(turn):
+        early = 1 - turn // (3 * near)
+        is_beside = early * (turn % 3 // 2)
+        is_across = early - is_beside
+        across, beside, close = turn // 3 * 2 + turn % 3, turn // 3, (turn + 1) % near
+        far_col = ((col // half + 1) % 2) * half + (col + across) % half
+        beside_col = col // half * half + ((col // quarter + 1) % 2) * quarter + (col + beside) % quarter
+        close_col = col // quarter * quarter + (col + close) % quarter
+        to_col = is_across * far_col + is_beside * beside_col + (1 - early) * close_col
+        step = is_across * (across // half) + is_beside * (beside // quarter) + (1 - early) * (close // quarter)
+        return (row + step) % row_count * col_count + to_col
+
+    def send(device):
+        return pltpu.make_async_remote_copy(
+            src_ref=outgoing.at[device], dst_ref=arrived.at[me], send_sem=send_sem.at[device],
+            recv_sem=recv_sem.at[me], device_id=place_of(device), device_id_type=MESH,
+        )
+
+    def receive(device):
+        return pltpu.make_async_remote_copy(
+            src_ref=outgoing.at[device], dst_ref=arrived.at[device], send_sem=send_sem.at[device],
+            recv_sem=recv_sem.at[device], device_id=place_of(device), device_id_type=MESH,
+        )
+
+    def send_sum(device):
+        return pltpu.make_async_remote_copy(
+            src_ref=sums.at[me], dst_ref=sums.at[me], send_sem=sum_send.at[device],
+            recv_sem=sum_recv.at[me], device_id=place_of(device), device_id_type=MESH,
+        )
+
+    def receive_sum(device):
+        return pltpu.make_async_remote_copy(
+            src_ref=sums.at[me], dst_ref=sums.at[device], send_sem=sum_send.at[device],
+            recv_sem=sum_recv.at[device], device_id=place_of(device), device_id_type=MESH,
+        )
+
+    barrier = pltpu.get_barrier_semaphore()
+
+    @pl.loop(1, devices)
+    def _(o):
+        pl.semaphore_signal(barrier, inc=1, device_id=place_of((me + o) % devices), device_id_type=MESH)
+
+    load_tiles(tiles, density, top, bottom, left, right, load_sem)
+    total[...] = jnp.zeros_like(total)
+    pl.semaphore_wait(barrier, devices - 1)
+
+    @pl.loop(0, devices * capacity)
+    def _(n):
+        turn, k = n // capacity, n % capacity
+        device = target(turn)
+        at = device * capacity + k
+        r, c = block_row[at], block_col[at]
+        cells = project_block(tiles[c, r], tiles[c + 1, r], tiles[c + 2, r], mask[at], rh, rl, ch, cl)
         total[...] += cells
-        out[i] = cells.astype(jnp.bfloat16)
-
-
-def project(order, mask, mask_cols, density, sides, band):
-    count = order.shape[0]
-    size = max(s for s in (16, 8, 4, 2, 1) if count % s == 0)
+        outgoing[device, k] = cells.astype(jnp.bfloat16)
+
+        @pl.when((k == 0) & (turn > 0))
+        def _():
+            send(target(turn - 1)).start()
+
+    sums[me] = jnp.sum(total[...].reshape(BS // 8, 8, BS), axis=0)
+    own = pltpu.make_async_copy(outgoing.at[me], arrived.at[me], load_sem.at[0])
+    own.start()
+    own.wait()
+
+    @pl.loop(1, devices)
+    def _(o):
+        send_sum((me + o) % devices).start()
+
+    @pl.loop(1, devices)
+    def _(o):
+        other = (me + o) % devices
+        send_sum(other).wait_send()
+        receive_sum(other).wait_recv()
+
+    volume[...] = jnp.sum(sums[...], axis=0)
+
+    @pl.loop(1, devices)
+    def _(o):
+        other = (me + o) % devices
+        send(other).wait_send()
+        receive(other).wait_recv()
+
+
+def exchange(order, mask, mask_cols, density, sides, band, sizes):
+    devices, capacity = order.shape
+    flat = order.reshape(-1)
     height, width = density.shape
     any_space = pl.BlockSpec(memory_space=pl.ANY)
     whole = pl.BlockSpec(memory_space=pltpu.VMEM)
     scalar = pl.BlockSpec(memory_space=pltpu.SMEM)
+    cells = devices * capacity * BS * BS
     return pl.pallas_call(
-        functools.partial(project_kernel, mask_cols),
-        grid=(count // size,),
+        functools.partial(exchange_kernel, sizes),
         out_shape=(
-            jax.ShapeDtypeStruct((count, BS, BS), jnp.bfloat16),
-            jax.ShapeDtypeStruct((BS, BS), jnp.float32),
+            jax.ShapeDtypeStruct((devices, capacity, BS, BS), jnp.bfloat16),
+            jax.ShapeDtypeStruct((8, BS), jnp.float32),
         ),
-        in_specs=[scalar] * 2 + [any_space] * 5 + [whole] * 4,
-        out_specs=(pl.BlockSpec((size, BS, BS), lambda i: (i, 0, 0)), pl.BlockSpec((BS, BS), lambda i: (0, 0))),
+        in_specs=[scalar] * 3 + [any_space] * 5 + [whole] * 4,
+        out_specs=(any_space, whole),
         scratch_shapes=[
-            pltpu.VMEM((height + 2 * RADIUS, width + 2 * BS), jnp.float32),
-            pltpu.SemaphoreType.DMA((5,)),
-        ],
-        compiler_params=pltpu.CompilerParams(vmem_limit_bytes=40 * MIB, dimension_semantics=("arbitrary",)),
-        cost_estimate=pl.CostEstimate(flops=count * BS * BS * 2000, bytes_accessed=density.size * 4, transcendentals=count * BS * BS),
-        name="project",
-    )(order, mask, density, *sides, *band)
+            pltpu.VMEM((width // BS + 2, height // BS, BS + 2 * RADIUS, BS), jnp.float32),
+            pltpu.VMEM((devices, capacity, BS, BS), jnp.bfloat16),
+            pltpu.VMEM((BS, BS), jnp.float32),
+            pltpu.VMEM((devices, 8, BS), jnp.float32),
+            pltpu.SemaphoreType.DMA((3 * (height // BS) + 2,)),
+        ]
+        + [pltpu.SemaphoreType.DMA((devices,))] * 4,
+        compiler_params=pltpu.CompilerParams(vmem_limit_bytes=48 * MIB, collective_id=0, has_side_effects=True),
+        cost_estimate=pl.CostEstimate(flops=cells * 2000, bytes_accessed=density.size * 4, transcendentals=cells),
+        name="exchange",
+    )(flat // mask_cols, flat % mask_cols, mask[flat], density, *sides, *band)
 
 
 def per_device(density, design_mask, rebalance):
     mask_rows, mask_cols = design_mask.shape
     count = mask_rows * mask_cols
-    row_count, col_count = lax.axis_size("row"), lax.axis_size("col")
-    devices = row_count * col_count
-    capacity = count // devices
-    order, slots = routing(rebalance, mask_rows, mask_cols, capacity)
-    sides = halos(density)
-    mask = design_mask.reshape(count)
-    band = bands()
-    cuts = sorted({0, max(1, capacity // 8), max(1, capacity // 2), capacity})
-    balanced, volume = None, 0.0
-    for a, b in zip(cuts[:-1], cuts[1:]):
-        blocks, cells = project(order[:, a:b].reshape(-1), mask, mask_cols, density, sides, band)
-        volume = volume + cells
-        arrived = lax.all_to_all(
-            blocks.reshape(devices, b - a, BS, BS), ("row", "col"), split_axis=0, concat_axis=0, tiled=True
-        )
-        balanced = place(arrived.reshape(-1, BS, BS), slots[:, a:b].reshape(-1), count, balanced)
-    total_volume = lax.psum(jnp.sum(volume), ("row", "col"))
-    constraint = total_volume / float(density.size * devices) / VOLUME_TARGET - 1.0
+    sizes = (lax.axis_size("row"), lax.axis_size("col"))
+    devices = sizes[0] * sizes[1]
+    order, slots = routing(rebalance, mask_rows, mask_cols, count // devices)
+    arrived, volume = exchange(
+        order, design_mask.reshape(count), mask_cols, density, halos(density), bands(), sizes
+    )
+    constraint = jnp.sum(volume) / float(density.size * devices) / VOLUME_TARGET - 1.0
+    balanced = place(arrived.reshape(count, BS, BS), slots.reshape(-1), count)
     return balanced, constraint
 
 

time: 316 us -> 250 us (0.79)
  blocking collectives: 112 us -> 0 us
  Pallas kernels: 142 us -> 213 us
  starting transfers between devices: 32.1 us -> 10.5 us
  local copies, waits for them, and re-layouts: 21.9 us -> 14.8 us
  waiting for transfers between devices: 0.83 us -> 5.57 us
    psum x1 -> x0, blocking collectives: 112 us -> none  [per_device(): total_volume = lax.psum(jnp.sum(volume), ('row', 'col'))]
    pallas_call x3 -> x1, Pallas kernels: 134 us -> 209 us  [exchange(): pl.pallas_call(functools.partial(exchange_kernel, sizes), out_shape=(jax....]
    all_to_all x3 -> x0, starting transfers between devices: 22.4 us -> none  [per_device(): lax.all_to_all(blocks.reshape(devices, b - a, BS, BS), ('row', 'col'), sp...]
    unnamed x48 -> x12, local copies, waits for them, and re-layouts: 13.8 us -> 7.07 us
    ppermute x4, waiting for transfers between devices: 0.83 us -> 5.57 us  [shift(): lax.ppermute(x, axis, [(i, i + step) for i in range(n) if 0 <= i + step <...]
    pallas_call x3 -> x1, Pallas kernels: 8.18 us -> 4.58 us  [place(): pl.pallas_call(functools.partial(place_kernel, groups), out_shape=jax.Sha...]
  transfers between devices with their start and end apart: 7 -> 4, of which waited for: 2 -> 1; matrix products, arithmetic and copies ran while one was open for 3% -> 3% of each run, Pallas kernels for 37% -> 0%
where the time goes in v2:
time: 250 us; the launch traced here: 248 us
  Pallas kernels  213 us (85%)
  local copies, waits for them, and re-layouts  14.8 us (6%)
  starting transfers between devices  10.5 us (4%)
  waiting for transfers between devices  5.57 us (2%)
  between operations  2.63 us (1%)
    pallas_call x1, Pallas kernels, exchange(): pl.pallas_call(functools.partial(exchange_kernel, sizes), out_shape=(jax....  209 us
    ppermute x4, starting transfers between devices, shift(): lax.ppermute(x, axis, [(i, i + step) for i in range(n) if 0 <= i + step <...  10.5 us
    unnamed x12, local copies, waits for them, and re-layouts  7.07 us
    ppermute x4, waiting for transfers between devices, shift(): lax.ppermute(x, axis, [(i, i + step) for i in range(n) if 0 <= i + step <...  5.57 us
  transfers between devices with their start and end apart: 4, of which 1 were waited for; matrix products, arithmetic and copies ran while one was open for 3% of the time, Pallas kernels for 0%

profile of v2, /device:TPU:0, one launch (start us, length us, event | category | flops | bytes accessed | tf_op | source)
XLA Modules:
  0.0 248.2 jit_solution(9384837266897811802)
XLA Ops:
  0.6 1.1 fusion.21
  1.7 1.3 collective-permute-start.1
  3.0 3.0 %collective-permute-start = (f32[16,4096]{1,0:T(8,128)S(1)}, f32[16,4096]{1,0:T(8,128)S(1)}, u32[]{:S(2)}, u32[]{:S(2)}) collective-permute-start(f32[16,4096]{1,0:T(8,128)S(1)} %get-tuple-element.27), channel_id=1, source_target_pairs={{0,8},{8,16},{16,24},{1,9},{9,17},{17,25},{2,10},{10,18},{18,26},{... | collective-permute-start | bytes 786440 | tf_op jit(solution)/shard_map/ppermute | solution.py:92
  6.1 0.8 reshape.55
  6.9 0.4 select_reduce_fusion
  7.6 1.4 fusion.20
  9.1 0.4 select_reduce_fusion.8
  9.5 0.8 reshape.58
  10.6 0.2 copy.49
  10.8 2.0 gather_fusion
  13.3 4.9 %collective-permute-start.2 = (f32[1056,16]{0,1:T(8,128)S(1)}, f32[1056,16]{0,1:T(8,128)S(1)}, u32[]{:S(2)}, u32[]{:S(2)}) collective-permute-start(f32[1056,16]{0,1:T(8,128)S(1)} %concatenate.6), channel_id=1, source_target_pairs={{0,1},{1,2},{2,3},{3,4},{4,5},{5,6},{6,7},{8,9},{9,10},{10,11},{11... | collective-permute-start | bytes 202760 | tf_op jit(solution)/shard_map/ppermute | solution.py:92
  18.3 1.3 collective-permute-start.3
  19.6 5.6 %collective-permute-done.3 = f32[1056,16]{0,1:T(8,128)S(1)} collective-permute-done((f32[1056,16]{0,1:T(8,128)S(1)}, f32[1056,16]{0,1:T(8,128)S(1)}, u32[]{:S(2)}, u32[]{:S(2)}) %collective-permute-start.3) | collective-permute-done | bytes 67616 | tf_op jit(solution)/shard_map/ppermute | solution.py:92
  25.2 0.2 copy.48
  25.4 0.2 copy.44
  25.7 0.2 pad.8.left
  25.9 0.8 copy-done.1
  26.7 0.8 copy-done.2
  27.6 0.8 copy-done.3
  28.4 0.8 copy-done.4
  29.2 208.6 %exchange.1 = (bf16[32,8,128,128]{3,2,1,0:T(8,128)(2,1)}, f32[8,128]{1,0:T(8,128)S(1)}) custom-call(s32[256]{0:T(256)S(1)} %get-tuple-element.33.block_row, s32[256]{0:T(256)S(1)} %get-tuple-element.32.block_col, s32[256]{0:T(256)S(1)} %gather_fusion, f32[1024,4096]{1,0:T(8,128)} %density.1, f32[32,16,128]{2,1,0:T(8,128)S(1)} %bitcast_bitcast_fusion.1.top, ...), custom_call_target="tpu_custom_call" | custom-call | flops 8388608000 | bytes 16777216 | tf_op jit(solution)/shard_map/exchange/pallas_call | solution.py:276
  237.9 0.6 reduce_sum.169
  239.1 3.4 %copy-done = bf16[32,8,128,128]{3,2,1,0:T(8,128)(2,1)S(1)} copy-done((bf16[32,8,128,128]{3,2,1,0:T(8,128)(2,1)S(1)}, bf16[32,8,128,128]{3,2,1,0:T(8,128)(2,1)}, u32[]{:S(2)}) %copy-start) | copy-done | bytes 8388632
  242.5 4.6 %place.1 = bf16[256,128,128]{2,1,0:T(8,128)(2,1)} custom-call(s32[256]{0:T(256)S(1)} %reshape.56.slots, bf16[256,128,128]{2,1,0:T(8,128)(2,1)S(1)} %bitcast.34), custom_call_target="tpu_custom_call" | custom-call | bytes 16777216 | tf_op jit(solution)/shard_map/place/pallas_call | solution.py:153
  (32 shorter events, 1.5 us)
Async XLA Ops:
  1.7 11.0 %collective-permute-start.1 = (f32[16,4096]{1,0:T(8,128)S(1)}, f32[16,4096]{1,0:T(8,128)S(1)}, u32[]{:S(2)}, u32[]{:S(2)}) collective-permute-start(f32[16,4096]{1,0:T(8,128)S(1)} %get-tuple-element.26), channel_id=1, source_target_pairs={{8,0},{16,8},{24,16},{9,1},{17,9},{25,17},{10,2},{18,10},{26,18},{... | collective-permute-start | bytes 786440 | tf_op jit(solution)/shard_map/ppermute | solution.py:92
  3.0 10.0 %collective-permute-start = (f32[16,4096]{1,0:T(8,128)S(1)}, f32[16,4096]{1,0:T(8,128)S(1)}, u32[]{:S(2)}, u32[]{:S(2)}) collective-permute-start(f32[16,4096]{1,0:T(8,128)S(1)} %get-tuple-element.27), channel_id=1, source_target_pairs={{0,8},{8,16},{16,24},{1,9},{9,17},{17,25},{2,10},{10,18},{18,26},{... | collective-permute-start | bytes 786440 | tf_op jit(solution)/shard_map/ppermute | solution.py:92
  13.3 12.2 %collective-permute-start.2 = (f32[1056,16]{0,1:T(8,128)S(1)}, f32[1056,16]{0,1:T(8,128)S(1)}, u32[]{:S(2)}, u32[]{:S(2)}) collective-permute-start(f32[1056,16]{0,1:T(8,128)S(1)} %concatenate.6), channel_id=1, source_target_pairs={{0,1},{1,2},{2,3},{3,4},{4,5},{5,6},{6,7},{8,9},{9,10},{10,11},{11... | collective-permute-start | bytes 202760 | tf_op jit(solution)/shard_map/ppermute | solution.py:92
  18.3 6.9 %collective-permute-start.3 = (f32[1056,16]{0,1:T(8,128)S(1)}, f32[1056,16]{0,1:T(8,128)S(1)}, u32[]{:S(2)}, u32[]{:S(2)}) collective-permute-start(f32[1056,16]{0,1:T(8,128)S(1)} %concatenate.7), channel_id=1, source_target_pairs={{1,0},{2,1},{3,2},{4,3},{5,4},{6,5},{7,6},{9,8},{10,9},{11,10},{12... | collective-permute-start | bytes 202760 | tf_op jit(solution)/shard_map/ppermute | solution.py:92
  25.9 0.8 copy-start.1
  26.7 0.8 copy-start.2
  27.6 0.8 copy-start.3
  28.4 0.8 copy-start.4
  239.1 3.4 %copy-start = (bf16[32,8,128,128]{3,2,1,0:T(8,128)(2,1)S(1)}, bf16[32,8,128,128]{3,2,1,0:T(8,128)(2,1)}, u32[]{:S(2)}) copy-start(bf16[32,8,128,128]{3,2,1,0:T(8,128)(2,1)} %get-tuple-element.4) | copy-start | bytes 25165828
